TPU v7x, 128 devices: a whole 4x4x4 slice. The times are simulated.
128 devices in a mesh: row: 8 (over y, core), col: 16 (over z, x).
Axes of the slice: x: 4, y: 4, z: 4, core: 2. Of those that a mesh axis runs over, the one named last changes fastest.
Arguments:
- activations: bfloat16 [8192, 7168], P('col', 'row'), may hold values from -6 to 6
- running_factor: float32 [7168, 7168], P('row', 'col'), as said below
- deltas: bfloat16 [64, 7168, 256], P('col', 'row'), may hold values from -1.5 to 1.5
- samples: int32 [64], P('col'), may hold values from 1 to 64
Outputs:
- updated_factor: float32 [7168, 7168], P('row', 'col')
- panel_factor: float32 [7168, 1024], P('row', 'col')
- solved_slab: float32 [7168, 256], P('row', 'col')
Inputs may be any that keep to these rules, and one draw needn't show every extreme that they name: running_factor is symmetric and its smallest eigenvalue is 0.5 or more.
All inputs are finite; a program needn't handle non-finite values.
Results may differ from a plain program's by a relative error of at most 0.0003.
Values may be sent and summed in bfloat16 or wider, within the bound.
No kernel may reach another device: no remote copies, remote signals or barrier semaphores. Data moves between devices by JAX's collectives and lax.ppermute only.
A program may use at most 128 MiB of HBM per device.

v0:
```python
import jax
import jax.numpy as jnp
from jax import lax
from jax.sharding import Mesh
from jax.sharding import PartitionSpec as P

TILE = 64
PANEL = 512
PANELS = 2
SHOTS = 64
COL = ("col_0", "col_1")
DECAY = 0.75
DAMPING = 0.05


def joined_along(parts, dim):
    parts = jnp.moveaxis(parts, 0, dim)
    lengths = parts.shape
    return parts.reshape(*lengths[:dim], lengths[dim] * lengths[dim + 1], *lengths[dim + 2 :])


def copy_for_each(shard, axis):
    size = lax.axis_size(axis)
    return lax.all_to_all(
        jnp.broadcast_to(shard[None], (size, *shard.shape)), axis, 0, 0, tiled=True
    )


def gather_directly(shard, axis, dim):
    return joined_along(copy_for_each(shard, axis), dim)


def from_root(shard, axis, root):
    return lax.dynamic_index_in_dim(lax.all_gather(shard, axis), root, 0, keepdims=False)


def filled_up(lines, size):
    spare = -len(lines) % size
    return jnp.pad(lines, [(0, spare)] + [(0, 0)] * (lines.ndim - 1))


def spread_2(shard, axis, root):
    lines = jnp.where(lax.axis_index(axis) == root, shard, jnp.zeros_like(shard)).reshape(
        -1, *shard.shape[1:][-1:]
    )
    padded = filled_up(lines, lax.axis_size(axis))
    own = lax.psum_scatter(padded, axis, scatter_dimension=0, tiled=True)
    return lax.all_gather(own, axis, axis=0, tiled=True)[: len(lines)].reshape(shard.shape)


def gather_axes(shard, axes, dim):
    whole = shard
    for number in range(len(axes) - 1, -1, -1):
        whole = lax.all_gather(whole, axes[number], axis=dim, tiled=True)
    return whole


def canon_rows(stored, group_size):
    trailing_shape = stored.shape[1:]
    blocks = stored.reshape((group_size, -1, TILE) + trailing_shape)
    return jnp.swapaxes(blocks, 0, 1).reshape((-1,) + trailing_shape)


def own_rows(canon, group_size, row_index):
    trailing_shape = canon.shape[1:]
    blocks = canon.reshape((-1, group_size, TILE) + trailing_shape)
    picked = lax.dynamic_index_in_dim(blocks, row_index, 1, keepdims=False)
    return picked.reshape((-1,) + trailing_shape)


def dot_high(left, right):
    return jnp.dot(left, right, precision=lax.Precision.HIGHEST)


def dot_transposed(left, right):
    return lax.dot_general(left, right, (((1,), (1,)), ((), ())), precision=lax.Precision.HIGHEST)


def diagonal_rows(panel_cols, panel_num, row_count):
    per_device = PANEL // TILE // row_count
    first_tile = panel_num * per_device
    local_rows = panel_cols[first_tile * TILE : (first_tile + per_device) * TILE]
    gathered = gather_directly(local_rows, "row", 0)
    return canon_rows(gathered, row_count)


def factor_rows(panel_cols, diag_block, first_row, row_global):
    lower_part = jnp.linalg.cholesky(diag_block)
    below = lax.linalg.triangular_solve(
        lower_part, panel_cols, left_side=False, lower=True, transpose_a=True
    )
    return (jnp.where((row_global >= first_row)[:, None], below, 0.0), lower_part)


def trailing_update(factor, stripe_cols, col_index, row_count, col_count):
    rounds = stripe_cols.reshape(-1, col_count // row_count, TILE, stripe_cols.shape[1])
    picked = lax.dynamic_index_in_dim(rounds, col_index // row_count, 1, keepdims=False)
    picked = picked.reshape(-1, stripe_cols.shape[1])
    column_rows = from_root(picked, "row", col_index % row_count)
    return factor - dot_transposed(stripe_cols, column_rows)


def on_device(activations, running_factor, deltas, samples):
    row_count = lax.axis_size("row")
    col_count = lax.axis_size(COL)
    row_index = lax.axis_index("row")
    col_index = lax.axis_index(COL)
    stripe = running_factor.shape[0]
    local_cols = running_factor.shape[1]
    spread = col_count // row_count
    row_local = jnp.arange(stripe, dtype=jnp.int32)
    col_local = jnp.arange(local_cols, dtype=jnp.int32)
    row_global = (row_local // TILE * row_count + row_index) * TILE + row_local % TILE
    col_global = (col_local // TILE * col_count + col_index) * TILE + col_local % TILE
    all_tokens = lax.all_gather(activations, COL, axis=0, tiled=True)
    tokens = all_tokens.shape[0]
    rounds = all_tokens.reshape(tokens, -1, spread, TILE)
    picked = lax.dynamic_index_in_dim(rounds, col_index // row_count, 2, keepdims=False).reshape(
        tokens, local_cols
    )
    column_feats = spread_2(picked, "row", col_index % row_count)
    gram_tile = lax.dot_general(
        all_tokens, column_feats, (((0,), (0,)), ((), ())), preferred_element_type=jnp.float32
    )
    identity = (row_global[:, None] == col_global[None, :]).astype(jnp.float32)
    factor = DECAY * running_factor + (1.0 - DECAY) / tokens * gram_tile + DAMPING * identity
    stripes = []
    lowers = []
    lead_width = PANELS * PANEL // col_count
    gathered = gather_axes(factor[:, :lead_width], COL, 1)
    early = jnp.swapaxes(gathered.reshape(stripe, col_count, -1, TILE), 1, 2).reshape(
        stripe, PANELS * PANEL
    )
    panel_zero = early[:, :PANEL]
    block_zero = diagonal_rows(panel_zero, 0, row_count)
    stripe_zero, lower_zero = factor_rows(panel_zero, block_zero, 0, row_global)
    per_rows = PANEL // row_count
    prior_rows, block_rows = (
        lax.all_gather(stripe_zero[per_rows : 2 * per_rows], "row", axis=0, tiled=True),
        lax.all_gather(
            early[per_rows : 2 * per_rows, PANEL : 2 * PANEL], "row", axis=0, tiled=True
        ),
    )
    prior = canon_rows(prior_rows, row_count)
    block_one = canon_rows(block_rows, row_count) - dot_transposed(prior, prior)
    panel_one = early[:, PANEL : 2 * PANEL] - dot_transposed(stripe_zero, prior)
    stripe_one, lower_one = factor_rows(panel_one, block_one, PANEL, row_global)
    factor = trailing_update(factor, stripe_zero, col_index, row_count, col_count)
    factor = trailing_update(factor, stripe_one, col_index, row_count, col_count)
    stripes = [stripe_zero, stripe_one]
    lowers = [lower_zero, lower_one]
    both_cols = jnp.concatenate(stripes, 1)
    width_out = both_cols.shape[1] // col_count
    panel_out = lax.dynamic_slice_in_dim(both_cols, col_index * width_out, width_out, 1)
    weights = (samples.astype(jnp.float32) / SHOTS).astype(jnp.bfloat16)
    partial_value = jnp.einsum("k,kmn->mn", weights, deltas, preferred_element_type=jnp.float32)
    slab_cols = lax.psum_scatter(partial_value, COL, scatter_dimension=1, tiled=True)
    done_rows = PANELS * PANEL // row_count
    per_rows = PANEL // row_count
    remainder = slab_cols
    pieces = []
    for panel_num in range(PANELS):
        rows_here = remainder[panel_num * per_rows : (panel_num + 1) * per_rows]
        gathered_rhs = lax.all_gather(rows_here, "row", axis=0, tiled=True)
        solved_part = lax.linalg.triangular_solve(
            lowers[panel_num], canon_rows(gathered_rhs, row_count), left_side=True, lower=True
        )
        remainder = remainder - dot_high(stripes[panel_num], solved_part)
        pieces.append(own_rows(solved_part, row_count, row_index))
    solved = jnp.concatenate(pieces + [remainder[done_rows:]], 0)
    return (factor, panel_out, solved)


def solution(mesh):
    finer = Mesh(mesh.devices.reshape(mesh.shape["row"], 4, 4), ("row", "col_0", "col_1"))
    return jax.shard_map(
        on_device,
        mesh=finer,
        in_specs=(P(COL, "row"), P("row", COL), P(COL, "row", None), P(COL)),
        out_specs=(P("row", COL), P("row", COL), P("row", COL)),
        check_vma=False,
    )
```

profile of v0, /device:TPU:1, one launch (start us, length us, event | category | flops | bytes accessed | tf_op | source)
XLA Modules:
  0.0 739.4 jit_solution(2623361062181280832)
XLA Ops:
  7.2 2.3 copy.23
  9.7 112.1 %all-gather.10.cloned.1.call-done = bf16[8192,896]{0,1:T(8,128)(2,1)} async-done(((bf16[512,896]{0,1:T(8,128)(2,1)}), bf16[8192,896]{0,1:T(8,128)(2,1)}) %all-gather.10.cloned.1.call-update) | async-done | bytes 14680080 | tf_op jit(solution)/shard_map/all_gather | solution.py:115
  121.8 6.5 dynamic-slice_select_fusion
  128.4 47.7 %reduce-scatter.2.cloned.1.call-done = bf16[1024,448]{0,1:T(8,128)(2,1)} async-done(((bf16[8192,448]{0,1:T(8,128)(2,1)}), bf16[1024,448]{0,1:T(8,128)(2,1)}) %reduce-scatter.2.cloned.1.call-update) | async-done | bytes 917520 | tf_op jit(solution)/shard_map/reduce_scatter | solution.py:47
  176.1 47.5 %all-gather.12.cloned.1.call-done = bf16[8192,448]{0,1:T(8,128)(2,1)} async-done(((bf16[1024,448]{0,1:T(8,128)(2,1)}), bf16[8192,448]{0,1:T(8,128)(2,1)}) %all-gather.12.cloned.1.call-update) | async-done | bytes 7340048 | tf_op jit(solution)/shard_map/all_gather | solution.py:48
  223.6 16.8 %fusion.2 = f32[896,448]{0,1:T(8,128)S(1)} fusion(f32[896,448]{0,1:T(8,128)} %param.10, bf16[8192,448]{0,1:T(8,128)(2,1)} %all-gather.12.cloned.1.call-done, bf16[8192,896]{0,1:T(8,128)(2,1)} %all-gather.10.cloned.1.call-done, s32[896]{0:T(1024)S(1)} %fusion.114, s32[448]{0:T(512)S(1)} %fusion.125), kind=kOutput, calls=%fused_computation.13 | convolution fusion | flops 6579077120 | bytes 25236736 | tf_op jit(solution)/shard_map/dot_general | solution.py:122
  240.5 13.0 %all_gather.32 = f32[896,256]{0,1:T(8,128)} all-gather(f32[896,64]{0,1:T(8,128)S(1)} %slice.257), channel_id=1, replica_groups=mesh['row'=8,'col_0'=4,'col_1'=4] {'col_1'}, dimensions={1}, use_global_device_ids=true | all-gather | bytes 1146880 | tf_op jit(solution)/shard_map/all_gather | solution.py:54
  253.5 45.9 %all-gather.14.cloned.1.call-done = f32[896,1024]{0,1:T(8,128)} async-done(((f32[896,256]{0,1:T(8,128)}), f32[896,1024]{0,1:T(8,128)}) %all-gather.14.cloned.1.call-update) | async-done | bytes 3670032 | tf_op jit(solution)/shard_map/all_gather | solution.py:54
  299.4 1.9 fusion.144
  301.3 1.7 copy.24
  303.0 2.0 broadcast_in_dim.34
  305.0 5.3 all-to-all-start
  311.3 13.9 %all-to-all-done = f32[8,64,512]{2,1,0:T(8,128)S(1)} async-done(((f32[8,64,512]{2,1,0:T(8,128)}), f32[8,64,512]{2,1,0:T(8,128)S(1)}, u32[]{:S(2)}, u32[]{:S(2)}) %all-to-all-start) | async-done | bytes 1048608 | tf_op jit(solution)/shard_map/all_to_all | solution.py:24
  328.9 11.7 %cholesky.286 = f32[128,128]{1,0:T(8,128)S(1)} custom-call(f32[128,128]{1,0:T(8,128)S(1)} %cholesky.426), custom_call_target="Cholesky" | custom-call | tf_op jit(solution)/shard_map/jit(cholesky)/cholesky | solution.py:88
  340.8 9.8 %custom-call.31 = f32[1,128,128]{1,2,0:T(8,128)S(1)} custom-call(f32[1,128,128]{2,1,0:T(8,128)S(1)} %get-tuple-element.79), custom_call_target="InvertDiagBlocksLowerTriangular" | custom-call | tf_op jit(solution)/shard_map/jit(cholesky)/cholesky | solution.py:88
  353.1 11.7 %cholesky.305 = f32[128,128]{1,0:T(8,128)S(1)} custom-call(f32[128,128]{1,0:T(8,128)S(1)} %cholesky.430), custom_call_target="Cholesky" | custom-call | tf_op jit(solution)/shard_map/jit(cholesky)/cholesky | solution.py:88
  364.9 10.0 %custom-call.32 = f32[1,128,128]{1,2,0:T(8,128)S(1)} custom-call(f32[1,128,128]{2,1,0:T(8,128)S(1)} %get-tuple-element.76), custom_call_target="InvertDiagBlocksLowerTriangular" | custom-call | tf_op jit(solution)/shard_map/jit(cholesky)/cholesky | solution.py:88
  376.4 11.7 %cholesky.326 = f32[128,128]{1,0:T(8,128)S(1)} custom-call(f32[128,128]{1,0:T(8,128)S(1)} %cholesky.435), custom_call_target="Cholesky" | custom-call | tf_op jit(solution)/shard_map/jit(cholesky)/cholesky | solution.py:88
  388.9 9.8 %custom-call.33 = f32[1,128,128]{1,2,0:T(8,128)S(1)} custom-call(f32[1,128,128]{2,1,0:T(8,128)S(1)} %get-tuple-element.73), custom_call_target="InvertDiagBlocksLowerTriangular" | custom-call | tf_op jit(solution)/shard_map/jit(cholesky)/cholesky | solution.py:88
  400.1 11.7 %cholesky.343 = f32[128,128]{1,0:T(8,128)S(1)} custom-call(f32[128,128]{1,0:T(8,128)S(1)} %convolution_subtract_fusion.10), custom_call_target="Cholesky" | custom-call | tf_op jit(solution)/shard_map/jit(cholesky)/cholesky | solution.py:88
  417.2 11.6 %while.8 = (s32[]{:T(128)}, f32[512,512]{1,0:T(8,128)}, s32[4,2]{0,1:T(2,128)S(1)}, f32[4,128,128]{2,1,0:T(8,128)S(1)}, s32[]{:T(128)}) while((s32[]{:T(128)}, f32[512,512]{1,0:T(8,128)}, s32[4,2]{0,1:T(2,128)S(1)}, f32[4,128,128]{2,1,0:T(8,128)S(1)}, s32[]{:T(128)}) %tuple.64), condition=%wide.while_cond, body=%wide.while_body.sunk | while | flops 2 | bytes 131181 | solution.py:89
  417.8 2.3 bitcast_dynamic-update-slice_fusion.4
  420.7 2.3 bitcast_dynamic-update-slice_fusion.4
  423.7 2.3 bitcast_dynamic-update-slice_fusion.4
  426.6 2.2 bitcast_dynamic-update-slice_fusion.4
  428.8 39.3 %custom-call.34 = f32[4,128,128]{1,2,0:T(8,128)S(1)} custom-call(f32[4,128,128]{2,1,0:T(8,128)S(1)} %get-tuple-element.34), custom_call_target="InvertDiagBlocksLowerTriangular" | custom-call | tf_op jit(solution)/shard_map/triangular_solve/custom-call.3 | solution.py:89
  468.1 1.6 fusion.36
  469.7 1.6 convolution_subtract_fusion.4
  471.9 1.8 convolution_subtract_fusion.2
  474.3 2.3 fusion.18
  479.6 1.5 fusion
  481.1 2.5 copy.52
  483.6 2.7 copy.29
  486.4 2.2 constant_dynamic-slice_fusion.5
  488.9 2.5 copy.32
  491.4 10.4 %all-gather.20.cloned.1.call-done = f32[512,512]{1,0:T(8,128)} async-done(((f32[64,512]{1,0:T(8,128)}), f32[512,512]{1,0:T(8,128)}) %all-gather.20.cloned.1.call-update) | async-done | bytes 1048592 | tf_op jit(solution)/shard_map/all_gather | solution.py:139
  501.8 3.8 convolution_subtract_fusion
  509.4 11.7 %cholesky.358 = f32[128,128]{1,0:T(8,128)S(1)} custom-call(f32[128,128]{1,0:T(8,128)S(1)} %cholesky.439), custom_call_target="Cholesky" | custom-call | tf_op jit(solution)/shard_map/jit(cholesky)/cholesky | solution.py:88
  522.2 9.8 %custom-call.35 = f32[1,128,128]{1,2,0:T(8,128)S(1)} custom-call(f32[1,128,128]{2,1,0:T(8,128)S(1)} %get-tuple-element.69), custom_call_target="InvertDiagBlocksLowerTriangular" | custom-call | tf_op jit(solution)/shard_map/jit(cholesky)/cholesky | solution.py:88
  532.1 1.9 constant_dynamic-update-slice_fusion
  535.3 12.1 %cholesky.377 = f32[128,128]{1,0:T(8,128)S(1)} custom-call(f32[128,128]{1,0:T(8,128)S(1)} %cholesky.443), custom_call_target="Cholesky" | custom-call | tf_op jit(solution)/shard_map/jit(cholesky)/cholesky | solution.py:88
  548.0 9.8 %custom-call.36 = f32[1,128,128]{1,2,0:T(8,128)S(1)} custom-call(f32[1,128,128]{2,1,0:T(8,128)S(1)} %get-tuple-element.66), custom_call_target="InvertDiagBlocksLowerTriangular" | custom-call | tf_op jit(solution)/shard_map/jit(cholesky)/cholesky | solution.py:88
  560.2 11.7 %cholesky.398 = f32[128,128]{1,0:T(8,128)S(1)} custom-call(f32[128,128]{1,0:T(8,128)S(1)} %cholesky.448), custom_call_target="Cholesky" | custom-call | tf_op jit(solution)/shard_map/jit(cholesky)/cholesky | solution.py:88
  572.6 9.8 %custom-call.37 = f32[1,128,128]{1,2,0:T(8,128)S(1)} custom-call(f32[1,128,128]{2,1,0:T(8,128)S(1)} %get-tuple-element.63), custom_call_target="InvertDiagBlocksLowerTriangular" | custom-call | tf_op jit(solution)/shard_map/jit(cholesky)/cholesky | solution.py:88
  583.2 1.5 convolution_subtract_fusion.9
  584.8 11.9 %cholesky.415 = f32[128,128]{1,0:T(8,128)S(1)} custom-call(f32[128,128]{1,0:T(8,128)S(1)} %convolution_subtract_fusion.9), custom_call_target="Cholesky" | custom-call | tf_op jit(solution)/shard_map/jit(cholesky)/cholesky | solution.py:88
  602.5 2.5 select_select_fusion
  605.0 12.0 %while.9 = (s32[]{:T(128)}, f32[512,512]{1,0:T(8,128)}, s32[4,2]{0,1:T(2,128)S(1)}, f32[4,128,128]{2,1,0:T(8,128)S(1)}, s32[]{:T(128)}) while((s32[]{:T(128)}, f32[512,512]{1,0:T(8,128)}, s32[4,2]{0,1:T(2,128)S(1)}, f32[4,128,128]{2,1,0:T(8,128)S(1)}, s32[]{:T(128)}) %tuple.88), condition=%wide.while_cond.clone, body=%wide.while_body.clone.sunk | while | flops 2 | bytes 131181 | solution.py:89
  605.7 2.3 bitcast_dynamic-update-slice_fusion.5
  608.7 2.3 bitcast_dynamic-update-slice_fusion.5
  611.8 2.3 bitcast_dynamic-update-slice_fusion.5
  614.8 2.3 bitcast_dynamic-update-slice_fusion.5
  617.8 40.1 %custom-call.38 = f32[4,128,128]{1,2,0:T(8,128)S(1)} custom-call(f32[4,128,128]{2,1,0:T(8,128)} %copy-done.8), custom_call_target="InvertDiagBlocksLowerTriangular" | custom-call | tf_op jit(solution)/shard_map/triangular_solve/custom-call.3 | solution.py:89
  657.9 5.6 slice_subtract_fusion
  666.1 1.6 convolution_subtract_fusion.1
  668.3 2.1 fusion.15
  672.3 2.8 copy.39
  675.2 2.2 constant_dynamic-slice_fusion.4
  679.4 13.1 %all-gather = f32[8,64,16]{1,2,0:T(8,128)S(1)} all-gather(f32[1,64,16]{1,2,0:T(8,128)S(1)} %dynamic-slice_bitcast_fusion), channel_id=1, replica_groups=mesh['row'=8,'col_0'=4,'col_1'=4] {'row'}, dimensions={0}, use_global_device_ids=true | all-gather | bytes 36864 | tf_op jit(solution)/shard_map/all_gather | solution.py:164
  696.9 2.6 convolution_subtract_fusion.11
  699.5 13.2 %all-gather.1 = f32[8,64,16]{1,2,0:T(8,128)S(1)} all-gather(f32[1,64,16]{1,2,0:T(8,128)S(1)} %slice_bitcast_fusion.24), channel_id=1, replica_groups=mesh['row'=8,'col_0'=4,'col_1'=4] {'row'}, dimensions={0}, use_global_device_ids=true | all-gather | bytes 36864 | tf_op jit(solution)/shard_map/all_gather | solution.py:164
  717.1 2.7 fusion.141
  721.2 4.9 fusion.30
  726.1 6.5 subtract_subtract_fusion
  (150 shorter events, 54.8 us)
Async XLA Ops:
  7.2 472.4 %copy-start = (bf16[4,896,256]{2,1,0:T(8,128)(2,1)S(1)}, bf16[4,896,256]{2,1,0:T(8,128)(2,1)}, u32[]{:S(2)}) copy-start(bf16[4,896,256]{2,1,0:T(8,128)(2,1)} %param.11) | copy-start | bytes 5505028
  7.2 114.6 %all-gather.10.cloned.1.call-start = ((), (), s32[]{:S(2)}) async-start(), calls=%async_computation.2 | async-start | bytes 15597568 | tf_op jit(solution)/shard_map/all_gather | solution.py:115
  9.6 166.5 %reduce-scatter.2.cloned.1.call-start = ((), (), s32[]{:S(2)}) async-start(), calls=%async_computation.3 | async-start | bytes 8257536 | tf_op jit(solution)/shard_map/reduce_scatter | solution.py:47
  128.3 95.3 %all-gather.12.cloned.1.call-start = ((), (), s32[]{:S(2)}) async-start(), calls=%async_computation.4 | async-start | bytes 8257536 | tf_op jit(solution)/shard_map/all_gather | solution.py:48
  176.1 123.3 %all-gather.14.cloned.1.call-start = ((), (), s32[]{:S(2)}) async-start(), calls=%async_computation.5 | async-start | bytes 4587520 | tf_op jit(solution)/shard_map/all_gather | solution.py:54
  240.4 62.6 %copy-start.6 = (f32[896,448]{0,1:T(8,128)}, f32[896,448]{0,1:T(8,128)S(1)}, u32[]{:S(2)}) copy-start(f32[896,448]{0,1:T(8,128)S(1)} %fusion.2) | copy-start | bytes 4816900
  305.0 5.3 copy-start.7
  305.0 20.2 %all-to-all-start = ((f32[8,64,512]{2,1,0:T(8,128)}), f32[8,64,512]{2,1,0:T(8,128)S(1)}, u32[]{:S(2)}, u32[]{:S(2)}) async-start(f32[8,64,512]{2,1,0:T(8,128)} %broadcast_in_dim.34), calls=%async_computation.1 | async-start | bytes 2097152 | tf_op jit(solution)/shard_map/all_to_all | solution.py:24
  310.3 178.6 %all-gather.18.cloned.1.call-start = ((), (), s32[]{:S(2)}) async-start(), calls=%async_computation.7 | async-start | bytes 1179648 | tf_op jit(solution)/shard_map/all_gather | solution.py:140
  311.1 190.7 %all-gather.20.cloned.1.call-start = ((), (), s32[]{:S(2)}) async-start(), calls=%async_computation.8 | async-start | bytes 1179648 | tf_op jit(solution)/shard_map/all_gather | solution.py:139
  327.9 1.0 copy-start.4
  477.2 2.4 copy-start.9
  477.3 1.2 copy-start.1
  479.5 199.2 %all-reduce.4.cloned.1.call-start = ((), (), s32[]{:S(2)}) async-start(), calls=%async_computation.10 | async-start | bytes 1835008
  483.6 237.7 %all-gather.16.cloned.1.call-start = ((), (), s32[]{:S(2)}) async-start(), calls=%async_computation.6 | async-start | bytes 8257536 | tf_op jit(solution)/shard_map/all_gather | solution.py:34
  488.6 237.5 %all-gather.22.cloned.1.call-start = ((), (), s32[]{:S(2)}) async-start(), calls=%async_computation.9 | async-start | bytes 8257536 | tf_op jit(solution)/shard_map/all_gather | solution.py:34
  508.4 1.0 copy-start.5
  583.2 74.7 %copy-start.3 = (f32[512,512]{1,0:T(8,128)S(1)}, f32[512,512]{1,0:T(8,128)}, u32[]{:S(2)}) copy-start(f32[512,512]{1,0:T(8,128)} %all-gather.20.cloned.1.call-done) | copy-start | bytes 3145732
  617.1 0.7 copy-start.8
  675.2 2.3 copy-start.10
  717.1 3.4 copy-start.2
Sparse Core Ops, SparseCore 0:
  10.7 111.0 all-gather.9
  128.4 47.5 reduce-scatter.1
  177.7 45.8 all-gather.11
  253.6 45.7 all-gather.13
  312.5 23.6 all-gather.17
  479.6 22.1 all-gather.19
  505.1 85.3 all-reduce.3
  592.2 46.6 all-gather.15
  677.5 45.4 all-gather.21
where the time goes:
time: 747 us; the launch traced here: 739 us
  waiting for transfers between devices  278 us (37%)
  other arithmetic  255 us (34%)
  matrix products  82.4 us (11%)
  local copies, waits for them, and re-layouts  58.1 us (8%)
  blocking collectives  39.3 us (5%)
  between operations  20.5 us (3%)
    another operation x29, other arithmetic, factor_rows(): lower_part = jnp.linalg.cholesky(diag_block)  160 us
    all_gather x1, waiting for transfers between devices, on_device(): all_tokens = lax.all_gather(activations, COL, axis=0, tiled=True)  112 us
    another operation x5, other arithmetic, factor_rows(): lax.linalg.triangular_solve(lower_part, panel_cols, left_side=False, lowe...  83 us
    reduce_scatter x1, waiting for transfers between devices, spread_2(): own = lax.psum_scatter(padded, axis, scatter_dimension=0, tiled=True)  47.7 us
    all_gather x1, waiting for transfers between devices, spread_2(): lax.all_gather(own, axis, axis=0, tiled=True)[:len(lines)]  47.5 us
    all_gather x1, waiting for transfers between devices, gather_axes(): whole = lax.all_gather(whole, axes[number], axis=dim, tiled=True)  45.9 us
    all_gather x2, blocking collectives, on_device(): gathered_rhs = lax.all_gather(rows_here, 'row', axis=0, tiled=True)  26.3 us
    another operation x27, local copies, waits for them, and re-layouts, factor_rows(): lax.linalg.triangular_solve(lower_part, panel_cols, left_side=False, lowe...  23.9 us
  transfers between devices with their start and end apart: 10, of which 6 were waited for; matrix products, arithmetic and copies ran while one was open for 48% of the time, Pallas kernels for 0%

commit v1 on v0

--- a/solution.py
+++ b/solution.py
@@ -45,7 +45,9 @@
     )
     padded = filled_up(lines, lax.axis_size(axis))
     own = lax.psum_scatter(padded, axis, scatter_dimension=0, tiled=True)
-    return lax.all_gather(own, axis, axis=0, tiled=True)[: len(lines)].reshape(shard.shape)
+    return jnp.concatenate(
+        lax.all_to_all(jnp.stack([own] * lax.axis_size(axis)), axis, 0, 0), axis=0
+    )[: len(lines)].reshape(shard.shape)
 
 
 def gather_axes(shard, axes, dim):

time: 747 us -> 801 us (1.072)
  waiting for transfers between devices: 278 us -> 312 us
  local copies, waits for them, and re-layouts: 58.1 us -> 70.4 us
    all_to_all x0 -> x1, waiting for transfers between devices: none -> 82.5 us  [spread_2(): lax.all_to_all(jnp.stack([own] * lax.axis_size(axis)), axis, 0, 0)]
    all_gather x1 -> x0, waiting for transfers between devices: 47.5 us -> none  [spread_2(): lax.all_gather(own, axis, axis=0, tiled=True)[:len(lines)]]
  transfers between devices with their start and end apart: 10 -> 10, of which waited for: 6 -> 6; matrix products, arithmetic and copies ran while one was open for 48% -> 45% of each run, Pallas kernels for 0% -> 0%
where the time goes in v1:
time: 801 us; the launch traced here: 793 us
  waiting for transfers between devices  312 us (39%)
  other arithmetic  255 us (32%)
  matrix products  82.4 us (10%)
  local copies, waits for them, and re-layouts  70.4 us (9%)
  blocking collectives  39.3 us (5%)
  between operations  20.8 us (3%)
  starting transfers between devices  11.8 us (1%)
    another operation x29, other arithmetic, factor_rows(): lower_part = jnp.linalg.cholesky(diag_block)  160 us
    all_gather x1, waiting for transfers between devices, on_device(): all_tokens = lax.all_gather(activations, COL, axis=0, tiled=True)  112 us
    another operation x5, other arithmetic, factor_rows(): lax.linalg.triangular_solve(lower_part, panel_cols, left_side=False, lowe...  83 us
    all_to_all x1, waiting for transfers between devices, spread_2(): lax.all_to_all(jnp.stack([own] * lax.axis_size(axis)), axis, 0, 0)  82.5 us
    reduce_scatter x1, waiting for transfers between devices, spread_2(): own = lax.psum_scatter(padded, axis, scatter_dimension=0, tiled=True)  47.7 us
    all_gather x1, waiting for transfers between devices, gather_axes(): whole = lax.all_gather(whole, axes[number], axis=dim, tiled=True)  45.5 us
    all_gather x2, blocking collectives, on_device(): gathered_rhs = lax.all_gather(rows_here, 'row', axis=0, tiled=True)  26.1 us
    another operation x27, local copies, waits for them, and re-layouts, factor_rows(): lax.linalg.triangular_solve(lower_part, panel_cols, left_side=False, lowe...  23.7 us
  transfers between devices with their start and end apart: 10, of which 6 were waited for; matrix products, arithmetic and copies ran while one was open for 45% of the time, Pallas kernels for 0%

profile of v1, /device:TPU:1, one launch (start us, length us, event | category | flops | bytes accessed | tf_op | source)
XLA Modules:
  0.0 792.5 jit_solution(16206990921896877767)
XLA Ops:
  7.2 2.3 copy.44
  9.7 112.1 %all-gather.9.cloned.1.call-done = bf16[8192,896]{0,1:T(8,128)(2,1)} async-done(((bf16[512,896]{0,1:T(8,128)(2,1)}), bf16[8192,896]{0,1:T(8,128)(2,1)}) %all-gather.9.cloned.1.call-update) | async-done | bytes 14680080 | tf_op jit(solution)/shard_map/all_gather | solution.py:117
  121.8 6.5 dynamic-slice_select_fusion
  128.3 47.7 %reduce-scatter.2.cloned.1.call-done = bf16[1024,448]{0,1:T(8,128)(2,1)} async-done(((bf16[8192,448]{0,1:T(8,128)(2,1)}), bf16[1024,448]{0,1:T(8,128)(2,1)}) %reduce-scatter.2.cloned.1.call-update) | async-done | bytes 917520 | tf_op jit(solution)/shard_map/reduce_scatter | solution.py:47
  176.1 5.1 stack.2
  181.2 5.9 all-to-all-start
  187.1 82.5 %all-to-all-done = bf16[8,1024,448]{1,2,0:T(8,128)(2,1)} async-done(((bf16[8,1024,448]{1,2,0:T(8,128)(2,1)}), bf16[8,1024,448]{1,2,0:T(8,128)(2,1)}, u32[]{:S(2)}, u32[]{:S(2)}) %all-to-all-start) | async-done | bytes 7340064 | tf_op jit(solution)/shard_map/all_to_all | solution.py:49
  269.6 7.3 copy.76
  276.9 16.8 %fusion.2 = f32[896,448]{0,1:T(8,128)S(1)} fusion(f32[896,448]{0,1:T(8,128)} %param.10, bf16[8192,448]{0,1:T(8,128)(2,1)} %bitcast.187, bf16[8192,896]{0,1:T(8,128)(2,1)} %all-gather.9.cloned.1.call-done, s32[896]{0:T(1024)S(1)} %fusion.114, s32[448]{0:T(512)S(1)} %fusion.125), kind=kOutput, calls=%fused_computation.13 | convolution fusion | flops 6579077120 | bytes 25236736 | tf_op jit(solution)/shard_map/dot_general | solution.py:124
  293.8 13.1 %all_gather.28 = f32[896,256]{0,1:T(8,128)} all-gather(f32[896,64]{0,1:T(8,128)S(1)} %slice.257), channel_id=1, replica_groups=mesh['row'=8,'col_0'=4,'col_1'=4] {'col_1'}, dimensions={1}, use_global_device_ids=true | all-gather | bytes 1146880 | tf_op jit(solution)/shard_map/all_gather | solution.py:56
  307.0 45.5 %all-gather.11.cloned.1.call-done = f32[896,1024]{0,1:T(8,128)} async-done(((f32[896,256]{0,1:T(8,128)}), f32[896,1024]{0,1:T(8,128)}) %all-gather.11.cloned.1.call-update) | async-done | bytes 3670032 | tf_op jit(solution)/shard_map/all_gather | solution.py:56
  352.4 1.9 fusion.144
  354.3 1.7 copy.46
  356.1 2.0 broadcast_in_dim.34
  358.1 5.3 all-to-all-start.1
  364.4 13.9 %all-to-all-done.1 = f32[8,64,512]{2,1,0:T(8,128)S(1)} async-done(((f32[8,64,512]{2,1,0:T(8,128)}), f32[8,64,512]{2,1,0:T(8,128)S(1)}, u32[]{:S(2)}, u32[]{:S(2)}) %all-to-all-start.1) | async-done | bytes 1048608 | tf_op jit(solution)/shard_map/all_to_all | solution.py:24
  382.0 11.7 %cholesky.286 = f32[128,128]{1,0:T(8,128)S(1)} custom-call(f32[128,128]{1,0:T(8,128)S(1)} %cholesky.426), custom_call_target="Cholesky" | custom-call | tf_op jit(solution)/shard_map/jit(cholesky)/cholesky | solution.py:90
  393.8 9.8 %custom-call.31 = f32[1,128,128]{1,2,0:T(8,128)S(1)} custom-call(f32[1,128,128]{2,1,0:T(8,128)S(1)} %get-tuple-element.79), custom_call_target="InvertDiagBlocksLowerTriangular" | custom-call | tf_op jit(solution)/shard_map/jit(cholesky)/cholesky | solution.py:90
  406.2 11.7 %cholesky.305 = f32[128,128]{1,0:T(8,128)S(1)} custom-call(f32[128,128]{1,0:T(8,128)S(1)} %cholesky.430), custom_call_target="Cholesky" | custom-call | tf_op jit(solution)/shard_map/jit(cholesky)/cholesky | solution.py:90
  417.9 10.0 %custom-call.32 = f32[1,128,128]{1,2,0:T(8,128)S(1)} custom-call(f32[1,128,128]{2,1,0:T(8,128)S(1)} %get-tuple-element.76), custom_call_target="InvertDiagBlocksLowerTriangular" | custom-call | tf_op jit(solution)/shard_map/jit(cholesky)/cholesky | solution.py:90
  429.5 11.7 %cholesky.326 = f32[128,128]{1,0:T(8,128)S(1)} custom-call(f32[128,128]{1,0:T(8,128)S(1)} %cholesky.435), custom_call_target="Cholesky" | custom-call | tf_op jit(solution)/shard_map/jit(cholesky)/cholesky | solution.py:90
  442.0 9.8 %custom-call.33 = f32[1,128,128]{1,2,0:T(8,128)S(1)} custom-call(f32[1,128,128]{2,1,0:T(8,128)S(1)} %get-tuple-element.73), custom_call_target="InvertDiagBlocksLowerTriangular" | custom-call | tf_op jit(solution)/shard_map/jit(cholesky)/cholesky | solution.py:90
  453.2 11.7 %cholesky.343 = f32[128,128]{1,0:T(8,128)S(1)} custom-call(f32[128,128]{1,0:T(8,128)S(1)} %convolution_subtract_fusion.10), custom_call_target="Cholesky" | custom-call | tf_op jit(solution)/shard_map/jit(cholesky)/cholesky | solution.py:90
  470.4 11.8 %while.8 = (s32[]{:T(128)}, f32[512,512]{1,0:T(8,128)}, s32[4,2]{0,1:T(2,128)S(1)}, f32[4,128,128]{2,1,0:T(8,128)S(1)}, s32[]{:T(128)}) while((s32[]{:T(128)}, f32[512,512]{1,0:T(8,128)}, s32[4,2]{0,1:T(2,128)S(1)}, f32[4,128,128]{2,1,0:T(8,128)S(1)}, s32[]{:T(128)}) %tuple.64), condition=%wide.while_cond, body=%wide.while_body.sunk | while | flops 2 | bytes 131181 | solution.py:91
  471.1 2.3 bitcast_dynamic-update-slice_fusion.4
  474.0 2.3 bitcast_dynamic-update-slice_fusion.4
  477.0 2.3 bitcast_dynamic-update-slice_fusion.4
  480.0 2.2 bitcast_dynamic-update-slice_fusion.4
  482.2 39.3 %custom-call.34 = f32[4,128,128]{1,2,0:T(8,128)S(1)} custom-call(f32[4,128,128]{2,1,0:T(8,128)S(1)} %get-tuple-element.34), custom_call_target="InvertDiagBlocksLowerTriangular" | custom-call | tf_op jit(solution)/shard_map/triangular_solve/custom-call.3 | solution.py:91
  523.1 1.6 convolution_subtract_fusion.4
  525.3 1.8 convolution_subtract_fusion.2
  527.7 2.3 fusion.18
  534.4 2.5 copy.74
  537.0 2.8 copy.51
  539.8 2.2 constant_dynamic-slice_fusion.5
  542.3 2.5 copy.54
  544.9 10.4 %all-gather.17.cloned.1.call-done = f32[512,512]{1,0:T(8,128)} async-done(((f32[64,512]{1,0:T(8,128)}), f32[512,512]{1,0:T(8,128)}) %all-gather.17.cloned.1.call-update) | async-done | bytes 1048592 | tf_op jit(solution)/shard_map/all_gather | solution.py:141
  555.2 3.8 convolution_subtract_fusion
  562.9 11.7 %cholesky.358 = f32[128,128]{1,0:T(8,128)S(1)} custom-call(f32[128,128]{1,0:T(8,128)S(1)} %cholesky.439), custom_call_target="Cholesky" | custom-call | tf_op jit(solution)/shard_map/jit(cholesky)/cholesky | solution.py:90
  575.8 9.8 %custom-call.35 = f32[1,128,128]{1,2,0:T(8,128)S(1)} custom-call(f32[1,128,128]{2,1,0:T(8,128)S(1)} %get-tuple-element.69), custom_call_target="InvertDiagBlocksLowerTriangular" | custom-call | tf_op jit(solution)/shard_map/jit(cholesky)/cholesky | solution.py:90
  585.6 1.9 constant_dynamic-update-slice_fusion
  588.8 12.1 %cholesky.377 = f32[128,128]{1,0:T(8,128)S(1)} custom-call(f32[128,128]{1,0:T(8,128)S(1)} %cholesky.443), custom_call_target="Cholesky" | custom-call | tf_op jit(solution)/shard_map/jit(cholesky)/cholesky | solution.py:90
  601.5 9.8 %custom-call.36 = f32[1,128,128]{1,2,0:T(8,128)S(1)} custom-call(f32[1,128,128]{2,1,0:T(8,128)S(1)} %get-tuple-element.66), custom_call_target="InvertDiagBlocksLowerTriangular" | custom-call | tf_op jit(solution)/shard_map/jit(cholesky)/cholesky | solution.py:90
  613.7 11.7 %cholesky.398 = f32[128,128]{1,0:T(8,128)S(1)} custom-call(f32[128,128]{1,0:T(8,128)S(1)} %cholesky.448), custom_call_target="Cholesky" | custom-call | tf_op jit(solution)/shard_map/jit(cholesky)/cholesky | solution.py:90
  626.1 9.8 %custom-call.37 = f32[1,128,128]{1,2,0:T(8,128)S(1)} custom-call(f32[1,128,128]{2,1,0:T(8,128)S(1)} %get-tuple-element.63), custom_call_target="InvertDiagBlocksLowerTriangular" | custom-call | tf_op jit(solution)/shard_map/jit(cholesky)/cholesky | solution.py:90
  638.2 11.9 %cholesky.415 = f32[128,128]{1,0:T(8,128)S(1)} custom-call(f32[128,128]{1,0:T(8,128)S(1)} %convolution_subtract_fusion.9), custom_call_target="Cholesky" | custom-call | tf_op jit(solution)/shard_map/jit(cholesky)/cholesky | solution.py:90
  655.9 2.4 select_select_fusion
  658.4 11.6 %while.9 = (s32[]{:T(128)}, f32[512,512]{1,0:T(8,128)}, s32[4,2]{0,1:T(2,128)S(1)}, f32[4,128,128]{2,1,0:T(8,128)S(1)}, s32[]{:T(128)}) while((s32[]{:T(128)}, f32[512,512]{1,0:T(8,128)}, s32[4,2]{0,1:T(2,128)S(1)}, f32[4,128,128]{2,1,0:T(8,128)S(1)}, s32[]{:T(128)}) %tuple.86), condition=%wide.while_cond.clone, body=%wide.while_body.clone.sunk | while | flops 2 | bytes 131181 | solution.py:91
  659.0 2.3 bitcast_dynamic-update-slice_fusion.5
  661.9 2.3 bitcast_dynamic-update-slice_fusion.5
  664.9 2.3 bitcast_dynamic-update-slice_fusion.5
  667.8 2.2 bitcast_dynamic-update-slice_fusion.5
  670.7 40.1 %custom-call.38 = f32[4,128,128]{1,2,0:T(8,128)S(1)} custom-call(f32[4,128,128]{2,1,0:T(8,128)} %copy-done.8), custom_call_target="InvertDiagBlocksLowerTriangular" | custom-call | tf_op jit(solution)/shard_map/triangular_solve/custom-call.3 | solution.py:91
  710.8 5.6 slice_subtract_fusion
  719.0 1.6 convolution_subtract_fusion.1
  721.2 2.1 fusion.15
  725.2 2.8 copy.61
  728.1 2.2 constant_dynamic-slice_fusion.4
  732.3 13.0 %all-gather = f32[8,64,16]{1,2,0:T(8,128)S(1)} all-gather(f32[1,64,16]{1,2,0:T(8,128)S(1)} %dynamic-slice_bitcast_fusion), channel_id=1, replica_groups=mesh['row'=8,'col_0'=4,'col_1'=4] {'row'}, dimensions={0}, use_global_device_ids=true | all-gather | bytes 36864 | tf_op jit(solution)/shard_map/all_gather | solution.py:166
  749.7 2.6 convolution_subtract_fusion.11
  752.4 13.1 %all-gather.1 = f32[8,64,16]{1,2,0:T(8,128)S(1)} all-gather(f32[1,64,16]{1,2,0:T(8,128)S(1)} %slice_bitcast_fusion.24), channel_id=1, replica_groups=mesh['row'=8,'col_0'=4,'col_1'=4] {'row'}, dimensions={0}, use_global_device_ids=true | all-gather | bytes 36864 | tf_op jit(solution)/shard_map/all_gather | solution.py:166
  769.8 2.7 fusion.141
  774.0 4.9 fusion.30
  778.9 6.5 subtract_subtract_fusion
  (151 shorter events, 59.4 us)
Async XLA Ops:
  7.2 525.8 %copy-start = (bf16[4,896,256]{2,1,0:T(8,128)(2,1)S(1)}, bf16[4,896,256]{2,1,0:T(8,128)(2,1)}, u32[]{:S(2)}) copy-start(bf16[4,896,256]{2,1,0:T(8,128)(2,1)} %param.11) | copy-start | bytes 5505028
  7.2 114.6 %all-gather.9.cloned.1.call-start = ((), (), s32[]{:S(2)}) async-start(), calls=%async_computation.3 | async-start | bytes 15597568 | tf_op jit(solution)/shard_map/all_gather | solution.py:117
  9.6 166.5 %reduce-scatter.2.cloned.1.call-start = ((), (), s32[]{:S(2)}) async-start(), calls=%async_computation.4 | async-start | bytes 8257536 | tf_op jit(solution)/shard_map/reduce_scatter | solution.py:47
  181.2 88.5 %all-to-all-start = ((bf16[8,1024,448]{1,2,0:T(8,128)(2,1)}), bf16[8,1024,448]{1,2,0:T(8,128)(2,1)}, u32[]{:S(2)}, u32[]{:S(2)}) async-start(bf16[8,1024,448]{1,2,0:T(8,128)(2,1)} %stack.2), calls=%async_computation.1 | async-start | bytes 14680064 | tf_op jit(solution)/shard_map/all_to_all | solution.py:49
  187.1 165.3 %all-gather.11.cloned.1.call-start = ((), (), s32[]{:S(2)}) async-start(), calls=%async_computation.5 | async-start | bytes 4587520 | tf_op jit(solution)/shard_map/all_gather | solution.py:56
  293.8 62.3 %copy-start.6 = (f32[896,448]{0,1:T(8,128)}, f32[896,448]{0,1:T(8,128)S(1)}, u32[]{:S(2)}) copy-start(f32[896,448]{0,1:T(8,128)S(1)} %fusion.2) | copy-start | bytes 4816900
  358.1 5.3 copy-start.7
  358.1 20.2 %all-to-all-start.1 = ((f32[8,64,512]{2,1,0:T(8,128)}), f32[8,64,512]{2,1,0:T(8,128)S(1)}, u32[]{:S(2)}, u32[]{:S(2)}) async-start(f32[8,64,512]{2,1,0:T(8,128)} %broadcast_in_dim.34), calls=%async_computation.2 | async-start | bytes 2097152 | tf_op jit(solution)/shard_map/all_to_all | solution.py:24
  363.3 179.0 %all-gather.15.cloned.1.call-start = ((), (), s32[]{:S(2)}) async-start(), calls=%async_computation.7 | async-start | bytes 1179648 | tf_op jit(solution)/shard_map/all_gather | solution.py:142
  364.1 191.1 %all-gather.17.cloned.1.call-start = ((), (), s32[]{:S(2)}) async-start(), calls=%async_computation.8 | async-start | bytes 1179648 | tf_op jit(solution)/shard_map/all_gather | solution.py:141
  381.0 1.0 copy-start.4
  530.6 2.4 copy-start.9
  530.7 1.2 copy-start.1
  532.9 198.7 %all-reduce.4.cloned.1.call-start = ((), (), s32[]{:S(2)}) async-start(), calls=%async_computation.10 | async-start | bytes 1835008
  537.0 237.0 %all-gather.13.cloned.1.call-start = ((), (), s32[]{:S(2)}) async-start(), calls=%async_computation.6 | async-start | bytes 8257536 | tf_op jit(solution)/shard_map/all_gather | solution.py:34
  542.0 236.8 %all-gather.19.cloned.1.call-start = ((), (), s32[]{:S(2)}) async-start(), calls=%async_computation.9 | async-start | bytes 8257536 | tf_op jit(solution)/shard_map/all_gather | solution.py:34
  561.9 1.0 copy-start.5
  636.7 74.1 %copy-start.3 = (f32[512,512]{1,0:T(8,128)S(1)}, f32[512,512]{1,0:T(8,128)}, u32[]{:S(2)}) copy-start(f32[512,512]{1,0:T(8,128)} %all-gather.17.cloned.1.call-done) | copy-start | bytes 3145732
  670.0 0.7 copy-start.8
  728.1 2.2 copy-start.10
  769.8 3.4 copy-start.2
Sparse Core Ops, SparseCore 0:
  10.7 111.0 all-gather.8
  128.5 47.5 reduce-scatter.1
  307.1 45.3 all-gather.10
  365.5 23.6 all-gather.14
  533.0 22.1 all-gather.16
  558.4 85.0 all-reduce.3
  645.2 46.5 all-gather.12
  730.4 45.5 all-gather.18
